TPU v7x, 32 devices: a whole 2x2x4 slice. The times are simulated.
32 devices in a mesh: dp: 8 (over z, x), param: 4 (over y, core).
Axes of the slice: x: 2, y: 2, z: 4, core: 2. Of those that a mesh axis runs over, the one named last changes fastest.
Arguments:
- ex_grads: bfloat16 [768, 5120], P('dp', 'param'), may hold values from -6 to 6
- tgt_grads: bfloat16 [2048, 5120], P('dp', 'param'), may hold values from -6 to 6
- projection: bfloat16 [5120, 4096], P('param'), may hold values from -0.078125 to 0.078125
- example_weight: float32 [768], P('param'), may hold values from 0.05 to 1
Outputs:
- scores: float32 [2048, 768], P('dp', 'param')
All inputs are finite; a program needn't handle non-finite values.
Results may differ from a plain program's by a relative error of at most 0.0078.
Values may be sent and summed in bfloat16 or wider, within the bound.
A program may use at most 192 MiB of HBM per device.

v0:
```python
import math
import jax
import jax.numpy as jnp
from jax import lax
from jax.sharding import PartitionSpec as P

ridge_value = 0.5


def with_ridge(block, first_row):
    row_ids = lax.broadcasted_iota(jnp.int32, block.shape, 0) + first_row
    col_ids = lax.broadcasted_iota(jnp.int32, block.shape, 1)
    return block + jnp.where(row_ids == col_ids, ridge_value, 0.0).astype(jnp.float32)


def on_device(ex_grads, tgt_grads, projection, example_weight):
    ex_rows = ex_grads.shape[0]
    columns = projection.shape[1]
    param_total = lax.axis_size("param")
    param_pos = lax.axis_index("param")
    replica_pos = lax.axis_index("dp")
    stacked = jnp.concatenate([ex_grads, tgt_grads], axis=0)
    contract_rows = (((0,), (1,)), ((), ()))
    feature_block = lax.psum_scatter(
        lax.dot_general(projection, stacked, contract_rows, preferred_element_type=jnp.float32),
        "param",
        scatter_dimension=0,
        tiled=True,
    )
    local_features = feature_block.astype(jnp.bfloat16)
    example_part = local_features[:, :ex_rows]
    contract_first = (((0,), (0,)), ((), ()))
    partial_value = lax.dot_general(
        local_features,
        lax.all_gather(example_part, "dp", axis=1, tiled=True),
        contract_first,
        preferred_element_type=jnp.float32,
    )
    examples = partial_value.shape[1]
    summed = lax.psum(partial_value, "param")
    kernel_block = with_ridge(summed[:ex_rows] / columns, replica_pos * ex_rows)
    kernel = lax.all_gather(kernel_block, "dp", axis=0, tiled=True)
    cross_terms = summed[ex_rows:] / columns
    factor = jnp.linalg.cholesky(kernel)
    forward = jax.scipy.linalg.solve_triangular(factor, cross_terms.T, lower=True)
    solved = jax.scipy.linalg.solve_triangular(factor, forward, lower=True, trans=1)
    block_cols = examples // param_total
    chosen = lax.dynamic_slice_in_dim(solved.T, param_pos * block_cols, block_cols, 1)
    return chosen * math.sqrt(columns) * example_weight[None, :]


def solution(mesh):
    placed = (P("dp", "param"), P("dp", "param"), P("param", None), P("param"))
    return jax.shard_map(
        on_device, mesh=mesh, in_specs=placed, out_specs=P("dp", "param"), check_vma=False
    )
```

profile of v0, /device:TPU:0, one launch (start us, length us, event | category | flops | bytes accessed | tf_op | source)
XLA Modules:
  0.0 462.6 jit_solution(8862410163447170017)
XLA Ops:
  6.5 10.7 %convolution_bitcast_fusion = f32[4096,352]{0,1:T(8,128)} fusion(bf16[1280,4096]{1,0:T(8,128)(2,1)} %param.6, bf16[256,1280]{1,0:T(8,128)(2,1)} %param.5, bf16[96,1280]{1,0:T(8,128)(2,1)} %param.4), kind=kOutput, calls=%fused_computation.2 | convolution fusion | flops 3692789760 | bytes 17154048 | tf_op jit(solution)/shard_map/dot_general | solution.py:25
  17.3 57.3 %reduce-scatter.2.cloned.1.call-done = f32[1024,352]{0,1:T(8,128)} async-done(((f32[4096,352]{0,1:T(8,128)}), f32[1024,352]{0,1:T(8,128)}) %reduce-scatter.2.cloned.1.call-update) | async-done | bytes 1441808 | tf_op jit(solution)/shard_map/reduce_scatter | solution.py:24
  74.6 1.5 convert_element_type.3
  76.1 0.7 slice.254
  76.9 44.3 %all-gather.3.cloned.1.call-done = bf16[1024,768]{0,1:T(8,128)(2,1)} async-done(((bf16[1024,96]{0,1:T(8,128)(2,1)}), bf16[1024,768]{0,1:T(8,128)(2,1)}) %all-gather.3.cloned.1.call-update) | async-done | bytes 1572880 | tf_op jit(solution)/shard_map/all_gather | solution.py:35
  121.2 3.2 fusion.85
  124.4 35.1 %all-reduce.3.cloned.1.call-done = f32[352,768]{1,0:T(8,128)} async-done(((f32[352,768]{1,0:T(8,128)}), f32[352,768]{1,0:T(8,128)}) %all-reduce.3.cloned.1.call-update) | async-done | bytes 1081360 | tf_op jit(solution)/shard_map/psum | solution.py:40
  159.6 1.8 fusion.37
  162.0 1.2 fusion.4
  163.2 50.6 %all-gather.5.cloned.1.call-done = f32[768,768]{1,0:T(8,128)} async-done(((f32[96,768]{1,0:T(8,128)}), f32[768,768]{1,0:T(8,128)}) %all-gather.5.cloned.1.call-update) | async-done | bytes 2359312 | tf_op jit(solution)/shard_map/all_gather | solution.py:42
  213.8 3.3 copy.7
  217.1 2.0 fusion
  219.1 1.4 copy-done.2
  220.5 11.7 %cholesky.165 = f32[128,128]{1,0:T(8,128)S(1)} custom-call(f32[128,128]{1,0:T(8,128)S(1)} %cholesky.424), custom_call_target="Cholesky" | custom-call | tf_op jit(solution)/shard_map/jit(cholesky)/cholesky | solution.py:44
  232.4 9.8 %custom-call.50 = f32[1,128,128]{1,2,0:T(8,128)S(1)} custom-call(f32[1,128,128]{2,1,0:T(8,128)S(1)} %get-tuple-element.38), custom_call_target="InvertDiagBlocksLowerTriangular" | custom-call | tf_op jit(solution)/shard_map/jit(cholesky)/cholesky | solution.py:44
  242.2 1.4 constant_dynamic-update-slice_fusion.20
  243.6 1.4 convolution_subtract_fusion
  245.7 12.5 %cholesky.188 = f32[128,128]{1,0:T(8,128)S(1)} custom-call(f32[128,128]{1,0:T(8,128)} %cholesky.428), custom_call_target="Cholesky" | custom-call | tf_op jit(solution)/shard_map/jit(cholesky)/cholesky | solution.py:44
  258.9 10.8 %custom-call.51 = f32[1,128,128]{1,2,0:T(8,128)S(1)} custom-call(f32[1,128,128]{2,1,0:T(8,128)} %get-tuple-element.35), custom_call_target="InvertDiagBlocksLowerTriangular" | custom-call | tf_op jit(solution)/shard_map/jit(cholesky)/cholesky | solution.py:44
  270.1 1.5 convolution_subtract_fusion.1
  271.6 11.7 %cholesky.354 = f32[128,128]{1,0:T(8,128)S(1)} custom-call(f32[128,128]{1,0:T(8,128)S(1)} %cholesky.433), custom_call_target="Cholesky" | custom-call | tf_op jit(solution)/shard_map/jit(cholesky)/cholesky | solution.py:44
  283.4 9.8 %custom-call.52 = f32[1,128,128]{1,2,0:T(8,128)S(1)} custom-call(f32[1,128,128]{2,1,0:T(8,128)S(1)} %get-tuple-element.32), custom_call_target="InvertDiagBlocksLowerTriangular" | custom-call | tf_op jit(solution)/shard_map/jit(cholesky)/cholesky | solution.py:44
  293.5 1.6 convolution_subtract_fusion.2
  295.1 12.1 %cholesky.373 = f32[128,128]{1,0:T(8,128)S(1)} custom-call(f32[128,128]{1,0:T(8,128)S(1)} %cholesky.438), custom_call_target="Cholesky" | custom-call | tf_op jit(solution)/shard_map/jit(cholesky)/cholesky | solution.py:44
  307.3 9.8 %custom-call.53 = f32[1,128,128]{1,2,0:T(8,128)S(1)} custom-call(f32[1,128,128]{2,1,0:T(8,128)S(1)} %get-tuple-element.29), custom_call_target="InvertDiagBlocksLowerTriangular" | custom-call | tf_op jit(solution)/shard_map/jit(cholesky)/cholesky | solution.py:44
  317.4 1.5 convolution_subtract_fusion.11
  318.9 11.7 %cholesky.392 = f32[128,128]{1,0:T(8,128)S(1)} custom-call(f32[128,128]{1,0:T(8,128)S(1)} %cholesky.443), custom_call_target="Cholesky" | custom-call | tf_op jit(solution)/shard_map/jit(cholesky)/cholesky | solution.py:44
  330.6 9.8 %custom-call.54 = f32[1,128,128]{1,2,0:T(8,128)S(1)} custom-call(f32[1,128,128]{2,1,0:T(8,128)S(1)} %get-tuple-element.26), custom_call_target="InvertDiagBlocksLowerTriangular" | custom-call | tf_op jit(solution)/shard_map/jit(cholesky)/cholesky | solution.py:44
  340.6 1.3 convolution_subtract_fusion.14
  342.0 11.9 %cholesky.410 = f32[128,128]{1,0:T(8,128)S(1)} custom-call(f32[128,128]{1,0:T(8,128)S(1)} %convolution_subtract_fusion.14), custom_call_target="Cholesky" | custom-call | tf_op jit(solution)/shard_map/jit(cholesky)/cholesky | solution.py:44
  353.9 0.7 compare_reduce_fusion.3
  355.9 0.7 compare_reduce_fusion
  361.0 1.6 select_select_fusion
  362.6 20.5 %while.1 = (s32[]{:T(128)}, f32[768,768]{1,0:T(8,128)}, s32[6,2]{0,1:T(2,128)S(1)}, f32[6,128,128]{2,1,0:T(8,128)}, s32[]{:T(128)}) while((s32[]{:T(128)}, f32[768,768]{1,0:T(8,128)}, s32[6,2]{0,1:T(2,128)S(1)}, f32[6,128,128]{2,1,0:T(8,128)}, s32[]{:T(128)}) %tuple.37), condition=%wide.while_cond, body=%wide.while_body.sunk | while | flops 2 | bytes 132205 | solution.py:46
  363.2 2.8 bitcast_dynamic-update-slice_fusion.2
  366.6 2.8 bitcast_dynamic-update-slice_fusion.2
  370.1 2.8 bitcast_dynamic-update-slice_fusion.2
  373.5 2.8 bitcast_dynamic-update-slice_fusion.2
  376.9 2.8 bitcast_dynamic-update-slice_fusion.2
  380.3 2.8 bitcast_dynamic-update-slice_fusion.2
  383.1 59.9 %custom-call.55 = f32[6,128,128]{1,2,0:T(8,128)S(1)} custom-call(f32[6,128,128]{2,1,0:T(8,128)} %get-tuple-element.12), custom_call_target="InvertDiagBlocksLowerTriangular" | custom-call | tf_op jit(solution)/shard_map/jit(_solve_triangular)/triangular_solve | solution.py:46
  443.3 1.2 convolution_subtract_fusion.13
  444.9 1.5 convolution_subtract_fusion.10
  446.7 0.8 convolution_subtract_fusion.9
  447.8 1.0 convolution_subtract_fusion.8
  449.2 1.3 convolution_subtract_fusion.7
  454.0 0.7 convolution_subtract_fusion.3
  455.1 0.8 multiply_bitcast_fusion
  (78 shorter events, 14.4 us)
Async XLA Ops:
  6.5 68.1 %reduce-scatter.2.cloned.1.call-start = ((), (), s32[]{:S(2)}) async-start(), calls=%async_computation.1 | async-start | bytes 7208960 | tf_op jit(solution)/shard_map/reduce_scatter | solution.py:24
  17.2 103.9 %all-gather.3.cloned.1.call-start = ((), (), s32[]{:S(2)}) async-start(), calls=%async_computation.2 | async-start | bytes 1769472 | tf_op jit(solution)/shard_map/all_gather | solution.py:35
  76.8 85.2 %copy-start.3 = (f32[192]{0:T(256)S(1)}, f32[192]{0:T(256)}, u32[]{:S(2)}) copy-start(f32[192]{0:T(256)} %param.7) | copy-start | bytes 2308
  76.8 82.7 %all-reduce.3.cloned.1.call-start = ((), (), s32[]{:S(2)}) async-start(), calls=%async_computation.3 | async-start | bytes 2162688 | tf_op jit(solution)/shard_map/psum | solution.py:40
  124.4 89.4 %all-gather.5.cloned.1.call-start = ((), (), s32[]{:S(2)}) async-start(), calls=%async_computation.4 | async-start | bytes 2654208 | tf_op jit(solution)/shard_map/all_gather | solution.py:42
  213.8 3.3 copy-start
  219.1 1.4 copy-start.2
  361.0 1.6 copy-start.4
  383.1 63.6 %copy-start.1 = (f32[768,768]{1,0:T(8,128)S(1)}, f32[768,768]{1,0:T(8,128)}, u32[]{:S(2)}) copy-start(f32[768,768]{1,0:T(8,128)} %get-tuple-element.104) | copy-start | bytes 7077892
Sparse Core Ops, SparseCore 0:
  17.4 57.2 reduce-scatter.1
  77.0 44.1 all-gather.2
  124.5 35.0 all-reduce.2
  161.6 52.1 all-gather.4
where the time goes:
time: 467 us; the launch traced here: 463 us
  other arithmetic  195 us (42%)
  waiting for transfers between devices  187 us (40%)
  matrix products  35.5 us (8%)
  local copies, waits for them, and re-layouts  26.8 us (6%)
  between operations  17.6 us (4%)
    another operation x22, other arithmetic, on_device(): factor = jnp.linalg.cholesky(kernel)  126 us
    another operation x3, other arithmetic, on_device(): jax.scipy.linalg.solve_triangular(factor, forward, lower=True, trans=1)  62.1 us
    reduce_scatter x1, waiting for transfers between devices, on_device(): lax.psum_scatter(lax.dot_general(projection, stacked, contract_rows, pref...  57.3 us
    all_gather x1, waiting for transfers between devices, on_device(): kernel = lax.all_gather(kernel_block, 'dp', axis=0, tiled=True)  50.6 us
    all_gather x1, waiting for transfers between devices, on_device(): lax.all_gather(example_part, 'dp', axis=1, tiled=True)  44.3 us
    psum x1, waiting for transfers between devices, on_device(): summed = lax.psum(partial_value, 'param')  35.1 us
    another operation x18, local copies, waits for them, and re-layouts  20.4 us
    dot_general x1, matrix products, on_device(): lax.dot_general(projection, stacked, contract_rows, preferred_element_typ...  10.7 us
  transfers between devices with their start and end apart: 4, of which 4 were waited for; matrix products, arithmetic and copies ran while one was open for 0% of the time, Pallas kernels for 0%

commit v1 on v0

--- a/solution.py
+++ b/solution.py
@@ -37,7 +37,9 @@
         preferred_element_type=jnp.float32,
     )
     examples = partial_value.shape[1]
-    summed = lax.psum(partial_value, "param")
+    summed = partial_value
+    for hop in (1, 2):
+        summed = summed + lax.ppermute(summed, "param", [(dev, dev ^ hop) for dev in range(4)])
     kernel_block = with_ridge(summed[:ex_rows] / columns, replica_pos * ex_rows)
     kernel = lax.all_gather(kernel_block, "dp", axis=0, tiled=True)
     cross_terms = summed[ex_rows:] / columns

time: 467 us -> 457 us (0.979)
  waiting for transfers between devices: 187 us -> 178 us
    psum x1 -> x0, waiting for transfers between devices: 35.1 us -> none  [on_device(): summed = lax.psum(partial_value, 'param')]
    ppermute x0 -> x2, waiting for transfers between devices: none -> 27.1 us  [on_device(): lax.ppermute(summed, 'param', [(dev, dev ^ hop) for dev in range(4)])]
  transfers between devices with their start and end apart: 4 -> 5, of which waited for: 4 -> 5; matrix products, arithmetic and copies ran while one was open for 0% -> 0% of each run, Pallas kernels for 0% -> 0%
where the time goes in v1:
time: 457 us; the launch traced here: 452 us
  other arithmetic  193 us (42%)
  waiting for transfers between devices  178 us (39%)
  matrix products  34.5 us (8%)
  local copies, waits for them, and re-layouts  26.8 us (6%)
  between operations  17.6 us (4%)
    another operation x22, other arithmetic, on_device(): factor = jnp.linalg.cholesky(kernel)  126 us
    another operation x3, other arithmetic, on_device(): jax.scipy.linalg.solve_triangular(factor, forward, lower=True, trans=1)  62.1 us
    reduce_scatter x1, waiting for transfers between devices, on_device(): lax.psum_scatter(lax.dot_general(projection, stacked, contract_rows, pref...  57.3 us
    all_gather x1, waiting for transfers between devices, on_device(): kernel = lax.all_gather(kernel_block, 'dp', axis=0, tiled=True)  49.7 us
    all_gather x1, waiting for transfers between devices, on_device(): lax.all_gather(example_part, 'dp', axis=1, tiled=True)  44.3 us
    ppermute x2, waiting for transfers between devices, on_device(): lax.ppermute(summed, 'param', [(dev, dev ^ hop) for dev in range(4)])  27.1 us
    another operation x18, local copies, waits for them, and re-layouts  20.4 us
    dot_general x1, matrix products, on_device(): lax.dot_general(projection, stacked, contract_rows, preferred_element_typ...  10.7 us
  transfers between devices with their start and end apart: 5, of which 5 were waited for; matrix products, arithmetic and copies ran while one was open for 0% of the time, Pallas kernels for 0%

profile of v1, /device:TPU:0, one launch (start us, length us, event | category | flops | bytes accessed | tf_op | source)
XLA Modules:
  0.0 452.4 jit_solution(6952331860185271510)
XLA Ops:
  6.5 10.7 %convolution_bitcast_fusion = f32[4096,352]{0,1:T(8,128)} fusion(bf16[1280,4096]{1,0:T(8,128)(2,1)} %param.6, bf16[256,1280]{1,0:T(8,128)(2,1)} %param.5, bf16[96,1280]{1,0:T(8,128)(2,1)} %param.4), kind=kOutput, calls=%fused_computation.2 | convolution fusion | flops 3692789760 | bytes 17154048 | tf_op jit(solution)/shard_map/dot_general | solution.py:25
  17.3 57.3 %reduce-scatter.2.cloned.1.call-done = f32[1024,352]{0,1:T(8,128)} async-done(((f32[4096,352]{0,1:T(8,128)}), f32[1024,352]{0,1:T(8,128)}) %reduce-scatter.2.cloned.1.call-update) | async-done | bytes 1441808 | tf_op jit(solution)/shard_map/reduce_scatter | solution.py:24
  74.6 1.5 convert_element_type.3
  76.9 44.3 %all-gather.3.cloned.1.call-done = bf16[1024,768]{0,1:T(8,128)(2,1)} async-done(((bf16[1024,96]{0,1:T(8,128)(2,1)}), bf16[1024,768]{0,1:T(8,128)(2,1)}) %all-gather.3.cloned.1.call-update) | async-done | bytes 1572880 | tf_op jit(solution)/shard_map/all_gather | solution.py:35
  121.2 2.2 fusion.90
  123.4 2.7 collective-permute-done
  126.3 1.5 collective-permute-start.1
  127.8 24.4 %collective-permute-done.1 = f32[352,768]{1,0:T(8,128)S(1)} collective-permute-done((f32[352,768]{1,0:T(8,128)S(1)}, f32[352,768]{1,0:T(8,128)S(1)}, u32[]{:S(2)}, u32[]{:S(2)}) %collective-permute-start.1) | collective-permute-done | bytes 1081376 | tf_op jit(solution)/shard_map/ppermute | solution.py:42
  152.4 0.8 fusion.40
  153.9 49.7 %all-gather.5.cloned.1.call-done = f32[768,768]{1,0:T(8,128)} async-done(((f32[96,768]{1,0:T(8,128)}), f32[768,768]{1,0:T(8,128)}) %all-gather.5.cloned.1.call-update) | async-done | bytes 2359312 | tf_op jit(solution)/shard_map/all_gather | solution.py:44
  203.5 3.3 copy.8
  206.9 2.0 fusion
  208.9 1.4 copy-done.2
  210.3 11.7 %cholesky.165 = f32[128,128]{1,0:T(8,128)S(1)} custom-call(f32[128,128]{1,0:T(8,128)S(1)} %cholesky.424), custom_call_target="Cholesky" | custom-call | tf_op jit(solution)/shard_map/jit(cholesky)/cholesky | solution.py:46
  222.2 9.8 %custom-call.50 = f32[1,128,128]{1,2,0:T(8,128)S(1)} custom-call(f32[1,128,128]{2,1,0:T(8,128)S(1)} %get-tuple-element.38), custom_call_target="InvertDiagBlocksLowerTriangular" | custom-call | tf_op jit(solution)/shard_map/jit(cholesky)/cholesky | solution.py:46
  232.0 1.4 constant_dynamic-update-slice_fusion.20
  233.4 1.4 convolution_subtract_fusion
  235.4 12.5 %cholesky.188 = f32[128,128]{1,0:T(8,128)S(1)} custom-call(f32[128,128]{1,0:T(8,128)} %cholesky.428), custom_call_target="Cholesky" | custom-call | tf_op jit(solution)/shard_map/jit(cholesky)/cholesky | solution.py:46
  248.6 10.8 %custom-call.51 = f32[1,128,128]{1,2,0:T(8,128)S(1)} custom-call(f32[1,128,128]{2,1,0:T(8,128)} %get-tuple-element.35), custom_call_target="InvertDiagBlocksLowerTriangular" | custom-call | tf_op jit(solution)/shard_map/jit(cholesky)/cholesky | solution.py:46
  259.8 1.5 convolution_subtract_fusion.1
  261.4 11.7 %cholesky.354 = f32[128,128]{1,0:T(8,128)S(1)} custom-call(f32[128,128]{1,0:T(8,128)S(1)} %cholesky.433), custom_call_target="Cholesky" | custom-call | tf_op jit(solution)/shard_map/jit(cholesky)/cholesky | solution.py:46
  273.1 9.8 %custom-call.52 = f32[1,128,128]{1,2,0:T(8,128)S(1)} custom-call(f32[1,128,128]{2,1,0:T(8,128)S(1)} %get-tuple-element.32), custom_call_target="InvertDiagBlocksLowerTriangular" | custom-call | tf_op jit(solution)/shard_map/jit(cholesky)/cholesky | solution.py:46
  283.3 1.6 convolution_subtract_fusion.2
  284.9 12.1 %cholesky.373 = f32[128,128]{1,0:T(8,128)S(1)} custom-call(f32[128,128]{1,0:T(8,128)S(1)} %cholesky.438), custom_call_target="Cholesky" | custom-call | tf_op jit(solution)/shard_map/jit(cholesky)/cholesky | solution.py:46
  297.0 9.8 %custom-call.53 = f32[1,128,128]{1,2,0:T(8,128)S(1)} custom-call(f32[1,128,128]{2,1,0:T(8,128)S(1)} %get-tuple-element.29), custom_call_target="InvertDiagBlocksLowerTriangular" | custom-call | tf_op jit(solution)/shard_map/jit(cholesky)/cholesky | solution.py:46
  307.1 1.5 convolution_subtract_fusion.7
  308.6 11.7 %cholesky.392 = f32[128,128]{1,0:T(8,128)S(1)} custom-call(f32[128,128]{1,0:T(8,128)S(1)} %cholesky.443), custom_call_target="Cholesky" | custom-call | tf_op jit(solution)/shard_map/jit(cholesky)/cholesky | solution.py:46
  320.4 9.8 %custom-call.54 = f32[1,128,128]{1,2,0:T(8,128)S(1)} custom-call(f32[1,128,128]{2,1,0:T(8,128)S(1)} %get-tuple-element.26), custom_call_target="InvertDiagBlocksLowerTriangular" | custom-call | tf_op jit(solution)/shard_map/jit(cholesky)/cholesky | solution.py:46
  330.4 1.3 convolution_subtract_fusion.9
  331.7 11.9 %cholesky.410 = f32[128,128]{1,0:T(8,128)S(1)} custom-call(f32[128,128]{1,0:T(8,128)S(1)} %convolution_subtract_fusion.9), custom_call_target="Cholesky" | custom-call | tf_op jit(solution)/shard_map/jit(cholesky)/cholesky | solution.py:46
  343.6 0.7 compare_reduce_fusion.3
  345.6 0.7 compare_reduce_fusion
  350.8 1.6 select_select_fusion
  352.4 20.5 %while.1 = (s32[]{:T(128)}, f32[768,768]{1,0:T(8,128)}, s32[6,2]{0,1:T(2,128)S(1)}, f32[6,128,128]{2,1,0:T(8,128)}, s32[]{:T(128)}) while((s32[]{:T(128)}, f32[768,768]{1,0:T(8,128)}, s32[6,2]{0,1:T(2,128)S(1)}, f32[6,128,128]{2,1,0:T(8,128)}, s32[]{:T(128)}) %tuple.37), condition=%wide.while_cond, body=%wide.while_body.sunk | while | flops 2 | bytes 132205 | solution.py:48
  353.0 2.8 bitcast_dynamic-update-slice_fusion.2
  356.4 2.8 bitcast_dynamic-update-slice_fusion.2
  359.8 2.8 bitcast_dynamic-update-slice_fusion.2
  363.2 2.8 bitcast_dynamic-update-slice_fusion.2
  366.7 2.8 bitcast_dynamic-update-slice_fusion.2
  370.1 2.8 bitcast_dynamic-update-slice_fusion.2
  372.8 59.9 %custom-call.55 = f32[6,128,128]{1,2,0:T(8,128)S(1)} custom-call(f32[6,128,128]{2,1,0:T(8,128)} %get-tuple-element.12), custom_call_target="InvertDiagBlocksLowerTriangular" | custom-call | tf_op jit(solution)/shard_map/jit(_solve_triangular)/triangular_solve | solution.py:48
  433.1 1.2 fusion.68
  434.6 1.5 fusion.45
  436.5 0.8 fusion.23
  437.6 1.0 fusion.8
  438.9 1.3 fusion.34
  443.8 0.7 convolution_subtract_fusion.3
  444.9 0.8 multiply_bitcast_fusion
  (81 shorter events, 15.5 us)
Async XLA Ops:
  6.5 68.1 %reduce-scatter.2.cloned.1.call-start = ((), (), s32[]{:S(2)}) async-start(), calls=%async_computation.1 | async-start | bytes 7208960 | tf_op jit(solution)/shard_map/reduce_scatter | solution.py:24
  17.2 103.9 %all-gather.3.cloned.1.call-start = ((), (), s32[]{:S(2)}) async-start(), calls=%async_computation.2 | async-start | bytes 1769472 | tf_op jit(solution)/shard_map/all_gather | solution.py:35
  76.8 126.7 %all-gather.5.cloned.1.call-start = ((), (), s32[]{:S(2)}) async-start(), calls=%async_computation.3 | async-start | bytes 2654208 | tf_op jit(solution)/shard_map/all_gather | solution.py:44
  123.3 2.8 collective-permute-start
  126.2 27.6 %copy-start.3 = (f32[192]{0:T(256)S(1)}, f32[192]{0:T(256)}, u32[]{:S(2)}) copy-start(f32[192]{0:T(256)} %param.7) | copy-start | bytes 2308
  126.3 26.0 %collective-permute-start.1 = (f32[352,768]{1,0:T(8,128)S(1)}, f32[352,768]{1,0:T(8,128)S(1)}, u32[]{:S(2)}, u32[]{:S(2)}) collective-permute-start(f32[352,768]{1,0:T(8,128)S(1)} %add.83), channel_id=1, source_target_pairs={{0,2},{1,3},{2,0},{3,1},{4,6},{5,7},{6,4},{7,5},{8,10},{9,11},{10,... | collective-permute-start | bytes 3244040 | tf_op jit(solution)/shard_map/ppermute | solution.py:42
  203.5 3.3 copy-start
  208.9 1.4 copy-start.2
  350.8 1.6 copy-start.4
  372.8 63.6 %copy-start.1 = (f32[768,768]{1,0:T(8,128)S(1)}, f32[768,768]{1,0:T(8,128)}, u32[]{:S(2)}) copy-start(f32[768,768]{1,0:T(8,128)} %get-tuple-element.103) | copy-start | bytes 7077892
Sparse Core Ops, SparseCore 0:
  17.4 57.2 reduce-scatter.1
  77.0 44.1 all-gather.2
  153.3 50.1 all-gather.4
